TPU v7x, 512 devices: a whole 4x4x16 slice. The times are simulated.
512 devices in a mesh: gx: 4 (over z_hi), gy: 8 (over y, core), gz: 16 (over x, z_lo).
Axes of the slice: x: 4, y: 4, z: 16 (z_hi: 4, z_lo: 4; z = z_hi * 4 + z_lo), core: 2. Of those that a mesh axis runs over, the one named last changes fastest.
Arguments:
- right_side: float32 [4, 8, 16, 6, 1024], P('gx', 'gy', 'gz'), may hold values from -18 to 18
- grain_diag: float32 [4, 8, 16, 6, 1024], P('gx', 'gy', 'gz'), may hold values from 0.05 to 0.5
- stiffness: float32 [4, 4], replicated, may hold values from 0.3 to 3
- contact_own: int32 [4, 8, 16, 3072], P('gx', 'gy', 'gz'), may hold values from 0 to 1023, as said below
- contact_slot: int32 [4, 8, 16, 3072], P('gx', 'gy', 'gz'), may hold values from 0 to 7679, as said below
- contact_type: int32 [4, 8, 16, 3072], P('gx', 'gy', 'gz'), may hold values from 0 to 4, as said below
- contact_normal: float32 [4, 8, 16, 3, 3072], P('gx', 'gy', 'gz'), may hold values from -1 to 1, as said below
- contact_radii: float32 [4, 8, 16, 2, 3072], P('gx', 'gy', 'gz'), may hold values from 0.4 to 1
Outputs:
- solution_field: float32 [4, 8, 16, 6, 1024], P('gx', 'gy', 'gz')
- residual: float32 [4, 8, 16, 6, 1024], P('gx', 'gy', 'gz')
Inputs may be any that keep to these rules, and one draw needn't show every extreme that they name: `contact_normal`: each normal has unit length. `contact_own`: in the first 2240 slots of a block the own grain differs from the partner; in the last 832 slots the own grain is one of the block's first 256 grains. `contact_slot`: the first 2240 slots of a block hold values below 1024; the slots 3072 - 832 + k * 32 to 2240 + (k + 1) * 32 - 1, for k = 0 to 25, hold values from 1024 + k * 256 to 1024 + (k + 1) * 256 - 1. `contact_type`: the value 4 marks an empty slot.
All inputs are finite; a program needn't handle non-finite values.
Results may differ from a plain program's by a relative error of at most 0.00018.
Values sent between devices are 32-bit elements; how exact they have to be, the bound alone decides.
A program may use at most 64 MiB of HBM per device.

v0:
```python
import jax
import jax.numpy as jnp
import numpy as np
from jax import lax
from jax.sharding import Mesh
from jax.sharding import PartitionSpec as P

ITERS = 4
GX_GY_GZ = ("gx", "gy_0", "gy_1", "gz_0", "gz_1")
GY = ("gy_0", "gy_1")
GZ = ("gz_0", "gz_1")


def one_axis_at_a_time(value, axes):
    for axis in axes:
        value = lax.psum(value, axis)
    return value


def with_halo(block, sides, width):
    for axis, dim in sides:
        count = lax.axis_size(axis)
        forward = [(i, i + 1) for i in range(count - 1)]
        forward.append((count - 1, 0))
        backward = [(target, source) for source, target in forward]
        low = lax.ppermute(
            lax.slice_in_dim(block, block.shape[dim] - width, None, axis=dim), axis, forward
        )
        high = lax.ppermute(lax.slice_in_dim(block, 0, width, axis=dim), axis, backward)
        block = jnp.concatenate([low, block, high], axis=dim)
    return block


def cross(left, right):
    return jnp.stack(
        [
            left[1] * right[2] - left[2] * right[1],
            left[2] * right[0] - left[0] * right[2],
            left[0] * right[1] - left[1] * right[0],
        ]
    )


def lookup(stiffness, ctype):
    total = jnp.zeros((4,) + ctype.shape, stiffness.dtype)
    for which in range(stiffness.shape[1]):
        total = total + stiffness[:, which : which + 1] * (ctype == which)[None].astype(
            stiffness.dtype
        )
    return total


def contact_response(first_u, second_u, normal, radii, coeff):
    normal_k, shear_k, roll_k, twist_k = (coeff[0], coeff[1], coeff[2], coeff[3])
    first_r, second_r = (radii[0], radii[1])
    delta = (
        second_u[:3]
        - second_r * cross(second_u[3:], normal)
        - first_u[:3]
        - first_r * cross(first_u[3:], normal)
    )
    along = jnp.sum(normal * delta, axis=0)
    force = shear_k * delta + (normal_k - shear_k) * along * normal
    theta = second_u[3:] - first_u[3:]
    twist = jnp.sum(normal * theta, axis=0)
    moment = roll_k * theta + (twist_k - roll_k) * twist * normal
    lever = cross(normal, force)
    on_first = jnp.concatenate([force, first_r * lever + moment], axis=0)
    on_second = jnp.concatenate([-force, second_r * lever - moment], axis=0)
    return (on_first, on_second)


def full_position(block):
    return block + (block >= 13).astype(jnp.int32)


def paired(residual, image):
    return (
        one_axis_at_a_time(jnp.sum(residual * residual), GX_GY_GZ),
        one_axis_at_a_time(jnp.sum(residual * image), GX_GY_GZ),
    )


def shards(
    right_side,
    grain_diag,
    stiffness,
    contact_own,
    contact_slot,
    contact_type,
    contact_normal,
    contact_radii,
):
    rhs = right_side[0, 0, 0]
    diag = grain_diag[0, 0, 0]
    grains = rhs.shape[1]
    rim = grains // 4
    owners = contact_own[0, 0, 0]
    slots = contact_slot[0, 0, 0]
    ctype = contact_type[0, 0, 0]
    normal = contact_normal[0, 0, 0]
    radii = contact_radii[0, 0, 0]
    coeff = lookup(stiffness, ctype)
    far_slot = slots >= grains
    rel = jnp.maximum(slots - grains, 0)
    ghost_column = full_position(rel // rim) * rim + rel % rim
    near_grain = jnp.where(far_slot, 0, slots)
    group_size = grains // 32
    remote_count = 26 * group_size
    packed = jnp.stack([owners[-remote_count:], slots[-remote_count:], ctype[-remote_count:]])[
        None, None, None
    ]
    theirs = with_halo(packed, (("gx", 0), (GY, 1), (GZ, 2)), 1).reshape(27, 3, 26, group_size)
    geometry = jnp.concatenate([normal[:, -remote_count:], radii[:, -remote_count:]], axis=0)[
        None, None, None
    ]
    their_geometry = with_halo(geometry, (("gx", 0), (GY, 1), (GZ, 2)), 1).reshape(
        27, 5, 26, group_size
    )
    counts = (lax.axis_size("gx"), lax.axis_size(GY), lax.axis_size(GZ))
    chosen_place = []
    chosen_group = []
    for place in range(27):
        for group in range(26):
            whole = group + (1 if group >= 13 else 0)
            back_x = (place // 9 - 1 + whole // 9 - 1) % counts[0] == 0
            back_y = (place // 3 % 3 - 1 + whole // 3 % 3 - 1) % counts[1] == 0
            back_z = (place % 3 - 1 + whole % 3 - 1) % counts[2] == 0
            if back_x and back_y and back_z:
                chosen_place.append(place)
                chosen_group.append(group)
    place_index = np.array(chosen_place, np.int32)
    group_index = np.array(chosen_group, np.int32)
    picked = theirs[place_index, :, group_index]
    picked_geometry = their_geometry[place_index, :, group_index]
    mirror_coeff = lookup(stiffness, picked[:, 2].reshape(-1))
    mirror_normal = jnp.moveaxis(picked_geometry[:, :3], 1, 0).reshape(3, -1)
    mirror_radii = jnp.moveaxis(picked_geometry[:, 3:], 1, 0).reshape(2, -1)
    mirror_place = jnp.asarray(np.repeat(place_index, group_size))
    mirror_column = mirror_place * rim + picked[:, 0].reshape(-1)
    mirror_mine = ((picked[:, 1] - grains) % rim).reshape(-1)

    def operate(field):
        rims = with_halo(field[None, None, None, :, :rim], (("gx", 0), (GY, 1), (GZ, 2)), 1)
        rim_flat = jnp.moveaxis(rims.reshape(27, 6, rim), 1, 0).reshape(6, 27 * rim)
        first_u = field[:, owners]
        second_u = jnp.where(far_slot[None], rim_flat[:, ghost_column], field[:, near_grain])
        on_first, on_second = contact_response(first_u, second_u, normal, radii, coeff)
        forces = jnp.zeros_like(field).at[:, owners].add(on_first)
        forces = forces.at[:, near_grain].add(jnp.where(far_slot[None], 0.0, on_second))
        their_u = rim_flat[:, mirror_column]
        unused, onto_mine = contact_response(
            their_u, field[:, mirror_mine], mirror_normal, mirror_radii, mirror_coeff
        )
        forces = forces.at[:, mirror_mine].add(onto_mine)
        return diag * field - forces

    solution_field = jnp.zeros_like(rhs)
    residual = rhs
    image = operate(residual)
    norm_now, product = paired(residual, image)
    alpha = norm_now / product
    direction, along = (residual, image)
    for step in range(ITERS):
        solution_field = solution_field + alpha * direction
        residual = residual - alpha * along
        if step + 1 < ITERS:
            image = operate(residual)
            norm_next, product = paired(residual, image)
            ratio = norm_next / norm_now
            alpha = norm_next / (product - ratio * norm_next / alpha)
            direction = residual + ratio * direction
            along = image + ratio * along
            norm_now = norm_next
    return (solution_field[None, None, None], residual[None, None, None])


def solution(mesh):
    torus = Mesh(
        mesh.devices.reshape(mesh.shape["gx"], 4, 2, 4, 4), ("gx", "gy_0", "gy_1", "gz_0", "gz_1")
    )
    placed = (
        P("gx", GY, GZ, None, None),
        P("gx", GY, GZ, None, None),
        P(),
        P("gx", GY, GZ, None),
        P("gx", GY, GZ, None),
        P("gx", GY, GZ, None),
        P("gx", GY, GZ, None, None),
        P("gx", GY, GZ, None, None),
    )
    return jax.shard_map(
        shards,
        mesh=torus,
        in_specs=placed,
        out_specs=(P("gx", GY, GZ, None, None), P("gx", GY, GZ, None, None)),
        check_vma=False,
    )
```

profile of v0, /device:TPU:8, one launch (start us, length us, event | category | flops | bytes accessed | tf_op | source)
XLA Modules:
  0.0 703.4 jit_solution(7459148122912372510)
XLA Ops:
  2.9 12.7 %collective-permute-start.7 = (s32[1,1,1,3,832]{4,3,2,1,0:T(4,128)S(1)}, s32[1,1,1,3,832]{4,3,2,1,0:T(4,128)S(1)}, u32[]{:S(2)}, u32[]{:S(2)}) collective-permute-start(s32[1,1,1,3,832]{4,3,2,1,0:T(4,128)S(1)} %add_bitcast_fusion.1), channel_id=1, source_target_pairs={{128,0},{256,128},{384,256},{0,384},{129,1},{257,129},{385,257},{1... | collective-permute-start | bytes 29960 | tf_op jit(solution)/shard_map/ppermute | solution.py:29
  102.8 10.1 %gather_fusion = f32[3072,6]{1,0:T(8,128)S(1)} fusion(f32[6,6912]{0,1:T(8,128)} %bitcast.453, s32[3072]{0:T(1024)S(1)} %broadcast_clamp_fusion.2), kind=kCustom, calls=%fused_computation | custom fusion | bytes 159744 | tf_op jit(solution)/shard_map/gather | solution.py:147
  116.2 17.4 %scatter_custom_fusion = f32[6,1024]{0,1:T(8,128)S(1)} fusion(s32[3072]{0:T(1024)S(1)} %bitcast.549, f32[3072,6]{1,0:T(8,128)} %copy.972, f32[]{:T(128)} %constant.32.clone.1), kind=kCustom, calls=%fused_computation.42 | custom fusion | flops 18432 | bytes 25088 | tf_op jit(solution)/shard_map/scatter-add | solution.py:149
  133.6 18.6 %scatter_fusion = f32[6,1024]{0,1:T(8,128)S(1)} fusion(f32[6,1024]{0,1:T(8,128)S(1)} %scatter_custom_fusion, s32[3072]{0:T(1024)S(1)} %bitcast.494, f32[3072,6]{1,0:T(8,128)S(1)} %copy.973), kind=kCustom, calls=%fused_computation.23 | custom fusion | flops 18432 | bytes 233472 | tf_op jit(solution)/shard_map/scatter-add | solution.py:150
  183.0 14.6 %all-reduce.15 = (f32[]{:T(128)}, f32[]{:T(128)}) all-reduce(f32[]{:T(128)} %get-tuple-element.40, f32[]{:T(128)} %get-tuple-element.39), channel_id=1, replica_groups=mesh['gx'=4,'gy_0'=4,'gy_1'=2,'gz_0'=4,'gz_1'=4] {'gx'}, use_global_device_ids=true, to_apply=%region_1.2 | all-reduce | flops 2 | bytes 16 | tf_op jit(solution)/shard_map/psum | solution.py:16
  197.6 10.0 %all-reduce.11 = (f32[]{:T(128)}, f32[]{:T(128)}) all-reduce(f32[]{:T(128)} %get-tuple-element.85, f32[]{:T(128)} %get-tuple-element.86), channel_id=1, replica_groups=mesh['gx'=4,'gy_0'=4,'gy_1'=2,'gz_0'=4,'gz_1'=4] {'gy_0'}, use_global_device_ids=true, to_apply=%region_2.3 | all-reduce | flops 2 | bytes 16 | tf_op jit(solution)/shard_map/psum | solution.py:16
  210.7 8.3 %all-reduce.7 = (f32[]{:T(128)}, f32[]{:T(128)}) all-reduce(f32[]{:T(128)} %get-tuple-element.93, f32[]{:T(128)} %get-tuple-element.94), channel_id=1, replica_groups=mesh['gx'=4,'gy_0'=4,'gy_1'=2,'gz_0'=4,'gz_1'=4] {'gz_0'}, use_global_device_ids=true, to_apply=%region_4.5 | all-reduce | flops 2 | bytes 16 | tf_op jit(solution)/shard_map/psum | solution.py:16
  219.0 15.4 %all-reduce.3 = (f32[]{:T(128)}, f32[]{:T(128)}) all-reduce(f32[]{:T(128)} %get-tuple-element.69, f32[]{:T(128)} %get-tuple-element.70), channel_id=1, replica_groups=mesh['gx'=4,'gy_0'=4,'gy_1'=2,'gz_0'=4,'gz_1'=4] {'gz_1'}, use_global_device_ids=true, to_apply=%region_5.6 | all-reduce | flops 2 | bytes 16 | tf_op jit(solution)/shard_map/psum | solution.py:16
  267.0 8.1 %gather_fusion.8 = f32[3072,6]{1,0:T(8,128)S(1)} fusion(f32[6,1024]{0,1:T(8,128)S(1)} %copy.993, s32[3072]{0:T(1024)S(1)} %get-tuple-element.240), kind=kCustom, calls=%fused_computation.8 | custom fusion | bytes 159744 | tf_op jit(solution)/shard_map/gather | solution.py:147
  282.2 10.1 %gather_fusion.7 = f32[3072,6]{1,0:T(8,128)S(1)} fusion(f32[6,6912]{0,1:T(8,128)} %bitcast.458, s32[3072]{0:T(1024)S(1)} %broadcast_clamp_fusion.2), kind=kCustom, calls=%fused_computation.7 | custom fusion | bytes 159744 | tf_op jit(solution)/shard_map/gather | solution.py:147
  294.6 17.0 %scatter_custom_fusion.3 = f32[6,1024]{0,1:T(8,128)S(1)} fusion(s32[3072]{0:T(1024)S(1)} %bitcast.550, f32[3072,6]{1,0:T(8,128)S(1)} %copy.998, f32[]{:T(128)} %constant.32.clone.1), kind=kCustom, calls=%fused_computation.40 | custom fusion | flops 18432 | bytes 24580 | tf_op jit(solution)/shard_map/scatter-add | solution.py:149
  312.2 18.4 %scatter_fusion.2 = f32[6,1024]{0,1:T(8,128)S(1)} fusion(f32[6,1024]{0,1:T(8,128)S(1)} %scatter_custom_fusion.3, s32[3072]{0:T(1024)S(1)} %bitcast.495, f32[3072,6]{1,0:T(8,128)S(1)} %copy.999), kind=kCustom, calls=%fused_computation.26 | custom fusion | flops 18432 | bytes 233472 | tf_op jit(solution)/shard_map/scatter-add | solution.py:150
  337.7 14.7 %all-reduce.14 = (f32[]{:T(128)}, f32[]{:T(128)}) all-reduce(f32[]{:T(128)} %get-tuple-element.36, f32[]{:T(128)} %get-tuple-element.35), channel_id=1, replica_groups=mesh['gx'=4,'gy_0'=4,'gy_1'=2,'gz_0'=4,'gz_1'=4] {'gx'}, use_global_device_ids=true, to_apply=%region_20.21 | all-reduce | flops 2 | bytes 16 | tf_op jit(solution)/shard_map/psum | solution.py:16
  352.4 10.2 %all-reduce.10 = (f32[]{:T(128)}, f32[]{:T(128)}) all-reduce(f32[]{:T(128)} %get-tuple-element.83, f32[]{:T(128)} %get-tuple-element.84), channel_id=1, replica_groups=mesh['gx'=4,'gy_0'=4,'gy_1'=2,'gz_0'=4,'gz_1'=4] {'gy_0'}, use_global_device_ids=true, to_apply=%region_21.22 | all-reduce | flops 2 | bytes 16 | tf_op jit(solution)/shard_map/psum | solution.py:16
  365.8 8.4 %all-reduce.6 = (f32[]{:T(128)}, f32[]{:T(128)}) all-reduce(f32[]{:T(128)} %get-tuple-element.91, f32[]{:T(128)} %get-tuple-element.92), channel_id=1, replica_groups=mesh['gx'=4,'gy_0'=4,'gy_1'=2,'gz_0'=4,'gz_1'=4] {'gz_0'}, use_global_device_ids=true, to_apply=%region_23.24 | all-reduce | flops 2 | bytes 16 | tf_op jit(solution)/shard_map/psum | solution.py:16
  374.2 13.5 %all-reduce.2 = (f32[]{:T(128)}, f32[]{:T(128)}) all-reduce(f32[]{:T(128)} %get-tuple-element.67, f32[]{:T(128)} %get-tuple-element.68), channel_id=1, replica_groups=mesh['gx'=4,'gy_0'=4,'gy_1'=2,'gz_0'=4,'gz_1'=4] {'gz_1'}, use_global_device_ids=true, to_apply=%region_24.25 | all-reduce | flops 2 | bytes 16 | tf_op jit(solution)/shard_map/psum | solution.py:16
  423.6 8.1 %gather_fusion.13 = f32[3072,6]{1,0:T(8,128)S(1)} fusion(f32[6,1024]{0,1:T(8,128)S(1)} %copy.1012, s32[3072]{0:T(1024)S(1)} %get-tuple-element.240), kind=kCustom, calls=%fused_computation.13 | custom fusion | bytes 159744 | tf_op jit(solution)/shard_map/gather | solution.py:147
  438.8 10.1 %gather_fusion.12 = f32[3072,6]{1,0:T(8,128)S(1)} fusion(f32[6,6912]{0,1:T(8,128)} %bitcast.460, s32[3072]{0:T(1024)S(1)} %broadcast_clamp_fusion.2), kind=kCustom, calls=%fused_computation.12 | custom fusion | bytes 159744 | tf_op jit(solution)/shard_map/gather | solution.py:147
  451.1 17.0 %scatter_custom_fusion.6 = f32[6,1024]{0,1:T(8,128)S(1)} fusion(s32[3072]{0:T(1024)S(1)} %bitcast.551, f32[3072,6]{1,0:T(8,128)S(1)} %copy.1017, f32[]{:T(128)} %constant.32.clone.1), kind=kCustom, calls=%fused_computation.38 | custom fusion | flops 18432 | bytes 24580 | tf_op jit(solution)/shard_map/scatter-add | solution.py:149
  468.7 18.4 %scatter_fusion.4 = f32[6,1024]{0,1:T(8,128)S(1)} fusion(f32[6,1024]{0,1:T(8,128)S(1)} %scatter_custom_fusion.6, s32[3072]{0:T(1024)S(1)} %bitcast.496, f32[3072,6]{1,0:T(8,128)S(1)} %copy.1018), kind=kCustom, calls=%fused_computation.29 | custom fusion | flops 18432 | bytes 233472 | tf_op jit(solution)/shard_map/scatter-add | solution.py:150
  494.2 14.6 %all-reduce.13 = (f32[]{:T(128)}, f32[]{:T(128)}) all-reduce(f32[]{:T(128)} %get-tuple-element.34, f32[]{:T(128)} %get-tuple-element.33), channel_id=1, replica_groups=mesh['gx'=4,'gy_0'=4,'gy_1'=2,'gz_0'=4,'gz_1'=4] {'gx'}, use_global_device_ids=true, to_apply=%region_39.40 | all-reduce | flops 2 | bytes 16 | tf_op jit(solution)/shard_map/psum | solution.py:16
  508.8 8.7 %all-reduce.9 = (f32[]{:T(128)}, f32[]{:T(128)}) all-reduce(f32[]{:T(128)} %get-tuple-element.81, f32[]{:T(128)} %get-tuple-element.82), channel_id=1, replica_groups=mesh['gx'=4,'gy_0'=4,'gy_1'=2,'gz_0'=4,'gz_1'=4] {'gy_0'}, use_global_device_ids=true, to_apply=%region_40.41 | all-reduce | flops 2 | bytes 16 | tf_op jit(solution)/shard_map/psum | solution.py:16
  520.5 8.3 %all-reduce.5 = (f32[]{:T(128)}, f32[]{:T(128)}) all-reduce(f32[]{:T(128)} %get-tuple-element.89, f32[]{:T(128)} %get-tuple-element.90), channel_id=1, replica_groups=mesh['gx'=4,'gy_0'=4,'gy_1'=2,'gz_0'=4,'gz_1'=4] {'gz_0'}, use_global_device_ids=true, to_apply=%region_42.43 | all-reduce | flops 2 | bytes 16 | tf_op jit(solution)/shard_map/psum | solution.py:16
  528.9 13.4 %all-reduce.1 = (f32[]{:T(128)}, f32[]{:T(128)}) all-reduce(f32[]{:T(128)} %get-tuple-element.65, f32[]{:T(128)} %get-tuple-element.66), channel_id=1, replica_groups=mesh['gx'=4,'gy_0'=4,'gy_1'=2,'gz_0'=4,'gz_1'=4] {'gz_1'}, use_global_device_ids=true, to_apply=%region_43.44 | all-reduce | flops 2 | bytes 16 | tf_op jit(solution)/shard_map/psum | solution.py:16
  577.2 8.1 %gather_fusion.18 = f32[3072,6]{1,0:T(8,128)S(1)} fusion(f32[6,1024]{0,1:T(8,128)S(1)} %copy.1031, s32[3072]{0:T(1024)S(1)} %get-tuple-element.240), kind=kCustom, calls=%fused_computation.18 | custom fusion | bytes 159744 | tf_op jit(solution)/shard_map/gather | solution.py:147
  592.5 10.1 %gather_fusion.17 = f32[3072,6]{1,0:T(8,128)S(1)} fusion(f32[6,6912]{0,1:T(8,128)} %bitcast.456, s32[3072]{0:T(1024)S(1)} %broadcast_clamp_fusion.2), kind=kCustom, calls=%fused_computation.17 | custom fusion | bytes 159744 | tf_op jit(solution)/shard_map/gather | solution.py:147
  604.8 17.0 %scatter_custom_fusion.9 = f32[6,1024]{0,1:T(8,128)S(1)} fusion(s32[3072]{0:T(1024)S(1)} %bitcast.552, f32[3072,6]{1,0:T(8,128)S(1)} %copy.1036, f32[]{:T(128)} %constant.32.clone.1), kind=kCustom, calls=%fused_computation.36 | custom fusion | flops 18432 | bytes 24580 | tf_op jit(solution)/shard_map/scatter-add | solution.py:149
  622.4 18.4 %scatter_fusion.6 = f32[6,1024]{0,1:T(8,128)S(1)} fusion(f32[6,1024]{0,1:T(8,128)S(1)} %scatter_custom_fusion.9, s32[3072]{0:T(1024)S(1)} %bitcast.497, f32[3072,6]{1,0:T(8,128)S(1)} %copy.1037), kind=kCustom, calls=%fused_computation.32 | custom fusion | flops 18432 | bytes 233472 | tf_op jit(solution)/shard_map/scatter-add | solution.py:150
  647.9 14.7 %all-reduce.12 = (f32[]{:T(128)}, f32[]{:T(128)}) all-reduce(f32[]{:T(128)} %get-tuple-element.32, f32[]{:T(128)} %get-tuple-element.31), channel_id=1, replica_groups=mesh['gx'=4,'gy_0'=4,'gy_1'=2,'gz_0'=4,'gz_1'=4] {'gx'}, use_global_device_ids=true, to_apply=%region_58.59 | all-reduce | flops 2 | bytes 16 | tf_op jit(solution)/shard_map/psum | solution.py:16
  662.6 10.1 %all-reduce.8 = (f32[]{:T(128)}, f32[]{:T(128)}) all-reduce(f32[]{:T(128)} %get-tuple-element.79, f32[]{:T(128)} %get-tuple-element.80), channel_id=1, replica_groups=mesh['gx'=4,'gy_0'=4,'gy_1'=2,'gz_0'=4,'gz_1'=4] {'gy_0'}, use_global_device_ids=true, to_apply=%region_59.60 | all-reduce | flops 2 | bytes 16 | tf_op jit(solution)/shard_map/psum | solution.py:16
  675.9 8.4 %all-reduce.4 = (f32[]{:T(128)}, f32[]{:T(128)}) all-reduce(f32[]{:T(128)} %get-tuple-element.87, f32[]{:T(128)} %get-tuple-element.88), channel_id=1, replica_groups=mesh['gx'=4,'gy_0'=4,'gy_1'=2,'gz_0'=4,'gz_1'=4] {'gz_0'}, use_global_device_ids=true, to_apply=%region_61.62 | all-reduce | flops 2 | bytes 16 | tf_op jit(solution)/shard_map/psum | solution.py:16
  684.2 13.5 %all-reduce = (f32[]{:T(128)}, f32[]{:T(128)}) all-reduce(f32[]{:T(128)} %get-tuple-element.63, f32[]{:T(128)} %get-tuple-element.64), channel_id=1, replica_groups=mesh['gx'=4,'gy_0'=4,'gy_1'=2,'gz_0'=4,'gz_1'=4] {'gz_1'}, use_global_device_ids=true, to_apply=%region_62.63 | all-reduce | flops 2 | bytes 16 | tf_op jit(solution)/shard_map/psum | solution.py:16
  (328 shorter events, 280.3 us)
Async XLA Ops:
  2.9 59.4 %collective-permute-start.7 = (s32[1,1,1,3,832]{4,3,2,1,0:T(4,128)S(1)}, s32[1,1,1,3,832]{4,3,2,1,0:T(4,128)S(1)}, u32[]{:S(2)}, u32[]{:S(2)}) collective-permute-start(s32[1,1,1,3,832]{4,3,2,1,0:T(4,128)S(1)} %add_bitcast_fusion.1), channel_id=1, source_target_pairs={{128,0},{256,128},{384,256},{0,384},{129,1},{257,129},{385,257},{1... | collective-permute-start | bytes 29960 | tf_op jit(solution)/shard_map/ppermute | solution.py:29
  15.7 47.1 %collective-permute-start.6 = (s32[1,1,1,3,832]{4,3,2,1,0:T(4,128)S(1)}, s32[1,1,1,3,832]{4,3,2,1,0:T(4,128)S(1)}, u32[]{:S(2)}, u32[]{:S(2)}) collective-permute-start(s32[1,1,1,3,832]{4,3,2,1,0:T(4,128)S(1)} %add_bitcast_fusion.1), channel_id=1, source_target_pairs={{0,128},{128,256},{256,384},{384,0},{1,129},{129,257},{257,385},{3... | collective-permute-start | bytes 29960 | tf_op jit(solution)/shard_map/ppermute | solution.py:26
  18.4 43.9 %collective-permute-start.1 = (f32[1,1,1,6,256]{4,3,2,1,0:T(8,128)S(1)}, f32[1,1,1,6,256]{4,3,2,1,0:T(8,128)S(1)}, u32[]{:S(2)}, u32[]{:S(2)}) collective-permute-start(f32[1,1,1,6,256]{4,3,2,1,0:T(8,128)S(1)} %slice_bitcast_fusion.5), channel_id=1, source_target_pairs={{128,0},{256,128},{384,256},{0,384},{129,1},{257,129},{385,257},{1... | collective-permute-start | bytes 18440 | tf_op jit(solution)/shard_map/ppermute | solution.py:29
  26.2 34.1 %collective-permute-start = (f32[1,1,1,6,256]{4,3,2,1,0:T(8,128)S(1)}, f32[1,1,1,6,256]{4,3,2,1,0:T(8,128)S(1)}, u32[]{:S(2)}, u32[]{:S(2)}) collective-permute-start(f32[1,1,1,6,256]{4,3,2,1,0:T(8,128)S(1)} %slice_bitcast_fusion.5), channel_id=1, source_target_pairs={{0,128},{128,256},{256,384},{384,0},{1,129},{129,257},{257,385},{3... | collective-permute-start | bytes 18440 | tf_op jit(solution)/shard_map/ppermute | solution.py:26
  29.8 40.5 %collective-permute-start.13 = (f32[1,1,1,5,832]{4,3,2,1,0:T(8,128)S(1)}, f32[1,1,1,5,832]{4,3,2,1,0:T(8,128)S(1)}, u32[]{:S(2)}, u32[]{:S(2)}) collective-permute-start(f32[1,1,1,5,832]{4,3,2,1,0:T(8,128)S(1)} %maximum_bitcast_fusion.4), channel_id=1, source_target_pairs={{128,0},{256,128},{384,256},{0,384},{129,1},{257,129},{385,257},{1... | collective-permute-start | bytes 49928 | tf_op jit(solution)/shard_map/ppermute | solution.py:29
  60.3 10.0 %collective-permute-start.12 = (f32[1,1,1,5,832]{4,3,2,1,0:T(8,128)S(1)}, f32[1,1,1,5,832]{4,3,2,1,0:T(8,128)S(1)}, u32[]{:S(2)}, u32[]{:S(2)}) collective-permute-start(f32[1,1,1,5,832]{4,3,2,1,0:T(8,128)S(1)} %maximum_bitcast_fusion.4), channel_id=1, source_target_pairs={{0,128},{128,256},{256,384},{384,0},{1,129},{129,257},{257,385},{3... | collective-permute-start | bytes 49928 | tf_op jit(solution)/shard_map/ppermute | solution.py:26
  62.3 9.8 %collective-permute-start.3 = (f32[3,1,1,6,256]{4,2,3,1,0:T(1,128)S(1)}, f32[3,1,1,6,256]{4,2,3,1,0:T(1,128)S(1)}, u32[]{:S(2)}, u32[]{:S(2)}) collective-permute-start(f32[3,1,1,6,256]{4,2,3,1,0:T(1,128)S(1)} %constant_dynamic-update-slice_fusion), channel_id=1, source_target_pairs={{16,0},{32,16},{48,32},{64,48},{80,64},{96,80},{112,96},{0,112},{1... | collective-permute-start | bytes 55304 | tf_op jit(solution)/shard_map/ppermute | solution.py:29
  62.3 9.8 %collective-permute-start.2 = (f32[3,1,1,6,256]{4,2,3,1,0:T(1,128)S(1)}, f32[3,1,1,6,256]{4,2,3,1,0:T(1,128)S(1)}, u32[]{:S(2)}, u32[]{:S(2)}) collective-permute-start(f32[3,1,1,6,256]{4,2,3,1,0:T(1,128)S(1)} %constant_dynamic-update-slice_fusion), channel_id=1, source_target_pairs={{0,16},{16,32},{32,48},{48,64},{64,80},{80,96},{96,112},{112,0},{1... | collective-permute-start | bytes 55304 | tf_op jit(solution)/shard_map/ppermute | solution.py:26
  62.8 15.1 %collective-permute-start.9 = (s32[3,1,1,3,832]{4,3,2,1,0:T(4,128)S(1)}, s32[3,1,1,3,832]{4,3,2,1,0:T(4,128)S(1)}, u32[]{:S(2)}, u32[]{:S(2)}) collective-permute-start(s32[3,1,1,3,832]{4,3,2,1,0:T(4,128)S(1)} %pad_add_fusion.2), channel_id=1, source_target_pairs={{16,0},{32,16},{48,32},{64,48},{80,64},{96,80},{112,96},{0,112},{1... | collective-permute-start | bytes 89864 | tf_op jit(solution)/shard_map/ppermute | solution.py:29
  70.3 9.6 %collective-permute-start.8 = (s32[3,1,1,3,832]{4,3,2,1,0:T(4,128)S(1)}, s32[3,1,1,3,832]{4,3,2,1,0:T(4,128)S(1)}, u32[]{:S(2)}, u32[]{:S(2)}) collective-permute-start(s32[3,1,1,3,832]{4,3,2,1,0:T(4,128)S(1)} %pad_add_fusion.2), channel_id=1, source_target_pairs={{0,16},{16,32},{32,48},{48,64},{64,80},{80,96},{96,112},{112,0},{1... | collective-permute-start | bytes 89864 | tf_op jit(solution)/shard_map/ppermute | solution.py:26
  70.4 17.4 %collective-permute-start.15 = (f32[3,1,1,5,832]{4,2,3,1,0:T(1,128)S(1)}, f32[3,1,1,5,832]{4,2,3,1,0:T(1,128)S(1)}, u32[]{:S(2)}, u32[]{:S(2)}) collective-permute-start(f32[3,1,1,5,832]{4,2,3,1,0:T(1,128)S(1)} %constant_dynamic-update-slice_fusion.3), channel_id=1, source_target_pairs={{16,0},{32,16},{48,32},{64,48},{80,64},{96,80},{112,96},{0,112},{1... | collective-permute-start | bytes 149768 | tf_op jit(solution)/shard_map/ppermute | solution.py:29
  72.1 17.6 %collective-permute-start.14 = (f32[3,1,1,5,832]{4,2,3,1,0:T(1,128)S(1)}, f32[3,1,1,5,832]{4,2,3,1,0:T(1,128)S(1)}, u32[]{:S(2)}, u32[]{:S(2)}) collective-permute-start(f32[3,1,1,5,832]{4,2,3,1,0:T(1,128)S(1)} %constant_dynamic-update-slice_fusion.3), channel_id=1, source_target_pairs={{0,16},{16,32},{32,48},{48,64},{64,80},{80,96},{96,112},{112,0},{1... | collective-permute-start | bytes 149768 | tf_op jit(solution)/shard_map/ppermute | solution.py:26
  72.2 26.2 %collective-permute-start.5 = (f32[3,3,1,6,256]{4,2,3,1,0:T(1,128)S(1)}, f32[3,3,1,6,256]{4,2,3,1,0:T(1,128)S(1)}, u32[]{:S(2)}, u32[]{:S(2)}) collective-permute-start(f32[3,3,1,6,256]{4,2,3,1,0:T(1,128)S(1)} %pad_maximum_fusion.6), channel_id=1, source_target_pairs={{1,0},{2,1},{3,2},{4,3},{5,4},{6,5},{7,6},{8,7},{9,8},{10,9},{11,1... | collective-permute-start | bytes 165896 | tf_op jit(solution)/shard_map/ppermute | solution.py:29
  77.9 22.4 %collective-permute-start.4 = (f32[3,3,1,6,256]{4,2,3,1,0:T(1,128)S(1)}, f32[3,3,1,6,256]{4,2,3,1,0:T(1,128)S(1)}, u32[]{:S(2)}, u32[]{:S(2)}) collective-permute-start(f32[3,3,1,6,256]{4,2,3,1,0:T(1,128)S(1)} %pad_maximum_fusion.6), channel_id=1, source_target_pairs={{0,1},{1,2},{2,3},{3,4},{4,5},{5,6},{6,7},{7,8},{8,9},{9,10},{10,1... | collective-permute-start | bytes 165896 | tf_op jit(solution)/shard_map/ppermute | solution.py:26
  79.9 72.3 %collective-permute-start.11 = (s32[3,3,1,3,832]{4,3,2,1,0:T(4,128)S(1)}, s32[3,3,1,3,832]{4,3,2,1,0:T(4,128)}, u32[]{:S(2)}, u32[]{:S(2)}) collective-permute-start(s32[3,3,1,3,832]{4,3,2,1,0:T(4,128)S(1)} %pad_add_fusion.1), channel_id=1, source_target_pairs={{1,0},{2,1},{3,2},{4,3},{5,4},{6,5},{7,6},{8,7},{9,8},{10,9},{11,1... | collective-permute-start | bytes 269576 | tf_op jit(solution)/shard_map/ppermute | solution.py:29
  87.8 64.4 %collective-permute-start.10 = (s32[3,3,1,3,832]{4,3,2,1,0:T(4,128)S(1)}, s32[3,3,1,3,832]{4,3,2,1,0:T(4,128)}, u32[]{:S(2)}, u32[]{:S(2)}) collective-permute-start(s32[3,3,1,3,832]{4,3,2,1,0:T(4,128)S(1)} %pad_add_fusion.1), channel_id=1, source_target_pairs={{0,1},{1,2},{2,3},{3,4},{4,5},{5,6},{6,7},{7,8},{8,9},{9,10},{10,1... | collective-permute-start | bytes 269576 | tf_op jit(solution)/shard_map/ppermute | solution.py:26
  90.5 74.3 %collective-permute-start.17 = (f32[3,3,1,5,832]{4,2,3,1,0:T(1,128)}, f32[3,3,1,5,832]{4,2,3,1,0:T(1,128)}, u32[]{:S(2)}, u32[]{:S(2)}) collective-permute-start(f32[3,3,1,5,832]{4,2,3,1,0:T(1,128)} %pad_maximum_fusion.5), channel_id=1, source_target_pairs={{1,0},{2,1},{3,2},{4,3},{5,4},{6,5},{7,6},{8,7},{9,8},{10,9},{11,1... | collective-permute-start | bytes 449288 | tf_op jit(solution)/shard_map/ppermute | solution.py:29
  98.3 66.5 %collective-permute-start.16 = (f32[3,3,1,5,832]{4,2,3,1,0:T(1,128)}, f32[3,3,1,5,832]{4,2,3,1,0:T(1,128)}, u32[]{:S(2)}, u32[]{:S(2)}) collective-permute-start(f32[3,3,1,5,832]{4,2,3,1,0:T(1,128)} %pad_maximum_fusion.5), channel_id=1, source_target_pairs={{0,1},{1,2},{2,3},{3,4},{4,5},{5,6},{6,7},{7,8},{8,9},{9,10},{10,1... | collective-permute-start | bytes 449288 | tf_op jit(solution)/shard_map/ppermute | solution.py:26
  235.8 9.8 %collective-permute-start.18 = (f32[1,1,1,6,256]{4,3,2,1,0:T(8,128)S(1)}, f32[1,1,1,6,256]{4,3,2,1,0:T(8,128)S(1)}, u32[]{:S(2)}, u32[]{:S(2)}) collective-permute-start(f32[1,1,1,6,256]{4,3,2,1,0:T(8,128)S(1)} %slice_bitcast_fusion.4), channel_id=1, source_target_pairs={{0,128},{128,256},{256,384},{384,0},{1,129},{129,257},{257,385},{3... | collective-permute-start | bytes 18440 | tf_op jit(solution)/shard_map/ppermute | solution.py:26
  240.1 9.5 %collective-permute-start.19 = (f32[1,1,1,6,256]{4,3,2,1,0:T(8,128)S(1)}, f32[1,1,1,6,256]{4,3,2,1,0:T(8,128)S(1)}, u32[]{:S(2)}, u32[]{:S(2)}) collective-permute-start(f32[1,1,1,6,256]{4,3,2,1,0:T(8,128)S(1)} %slice_bitcast_fusion.4), channel_id=1, source_target_pairs={{128,0},{256,128},{384,256},{0,384},{129,1},{257,129},{385,257},{1... | collective-permute-start | bytes 18440 | tf_op jit(solution)/shard_map/ppermute | solution.py:29
  259.0 16.8 %collective-permute-start.23 = (f32[3,3,1,6,256]{4,2,3,1,0:T(1,128)S(1)}, f32[3,3,1,6,256]{4,2,3,1,0:T(1,128)S(1)}, u32[]{:S(2)}, u32[]{:S(2)}) collective-permute-start(f32[3,3,1,6,256]{4,2,3,1,0:T(1,128)S(1)} %pad_maximum_fusion.7), channel_id=1, source_target_pairs={{1,0},{2,1},{3,2},{4,3},{5,4},{6,5},{7,6},{8,7},{9,8},{10,9},{11,1... | collective-permute-start | bytes 165896 | tf_op jit(solution)/shard_map/ppermute | solution.py:29
  260.9 14.9 %collective-permute-start.22 = (f32[3,3,1,6,256]{4,2,3,1,0:T(1,128)S(1)}, f32[3,3,1,6,256]{4,2,3,1,0:T(1,128)S(1)}, u32[]{:S(2)}, u32[]{:S(2)}) collective-permute-start(f32[3,3,1,6,256]{4,2,3,1,0:T(1,128)S(1)} %pad_maximum_fusion.7), channel_id=1, source_target_pairs={{0,1},{1,2},{2,3},{3,4},{4,5},{5,6},{6,7},{7,8},{8,9},{9,10},{10,1... | collective-permute-start | bytes 165896 | tf_op jit(solution)/shard_map/ppermute | solution.py:26
  392.2 9.8 %collective-permute-start.24 = (f32[1,1,1,6,256]{4,3,2,1,0:T(8,128)S(1)}, f32[1,1,1,6,256]{4,3,2,1,0:T(8,128)S(1)}, u32[]{:S(2)}, u32[]{:S(2)}) collective-permute-start(f32[1,1,1,6,256]{4,3,2,1,0:T(8,128)S(1)} %slice_bitcast_fusion.3), channel_id=1, source_target_pairs={{0,128},{128,256},{256,384},{384,0},{1,129},{129,257},{257,385},{3... | collective-permute-start | bytes 18440 | tf_op jit(solution)/shard_map/ppermute | solution.py:26
  396.5 9.5 %collective-permute-start.25 = (f32[1,1,1,6,256]{4,3,2,1,0:T(8,128)S(1)}, f32[1,1,1,6,256]{4,3,2,1,0:T(8,128)S(1)}, u32[]{:S(2)}, u32[]{:S(2)}) collective-permute-start(f32[1,1,1,6,256]{4,3,2,1,0:T(8,128)S(1)} %slice_bitcast_fusion.3), channel_id=1, source_target_pairs={{128,0},{256,128},{384,256},{0,384},{129,1},{257,129},{385,257},{1... | collective-permute-start | bytes 18440 | tf_op jit(solution)/shard_map/ppermute | solution.py:29
  405.9 9.4 %collective-permute-start.27 = (f32[3,1,1,6,256]{4,2,3,1,0:T(1,128)S(1)}, f32[3,1,1,6,256]{4,2,3,1,0:T(1,128)S(1)}, u32[]{:S(2)}, u32[]{:S(2)}) collective-permute-start(f32[3,1,1,6,256]{4,2,3,1,0:T(1,128)S(1)} %constant_dynamic-update-slice_fusion.9), channel_id=1, source_target_pairs={{16,0},{32,16},{48,32},{64,48},{80,64},{96,80},{112,96},{0,112},{1... | collective-permute-start | bytes 55304 | tf_op jit(solution)/shard_map/ppermute | solution.py:29
  415.4 17.0 %collective-permute-start.29 = (f32[3,3,1,6,256]{4,2,3,1,0:T(1,128)S(1)}, f32[3,3,1,6,256]{4,2,3,1,0:T(1,128)S(1)}, u32[]{:S(2)}, u32[]{:S(2)}) collective-permute-start(f32[3,3,1,6,256]{4,2,3,1,0:T(1,128)S(1)} %pad_maximum_fusion.8), channel_id=1, source_target_pairs={{1,0},{2,1},{3,2},{4,3},{5,4},{6,5},{7,6},{8,7},{9,8},{10,9},{11,1... | collective-permute-start | bytes 165896 | tf_op jit(solution)/shard_map/ppermute | solution.py:29
  417.3 15.1 %collective-permute-start.28 = (f32[3,3,1,6,256]{4,2,3,1,0:T(1,128)S(1)}, f32[3,3,1,6,256]{4,2,3,1,0:T(1,128)S(1)}, u32[]{:S(2)}, u32[]{:S(2)}) collective-permute-start(f32[3,3,1,6,256]{4,2,3,1,0:T(1,128)S(1)} %pad_maximum_fusion.8), channel_id=1, source_target_pairs={{0,1},{1,2},{2,3},{3,4},{4,5},{5,6},{6,7},{7,8},{8,9},{9,10},{10,1... | collective-permute-start | bytes 165896 | tf_op jit(solution)/shard_map/ppermute | solution.py:26
  546.1 9.8 %collective-permute-start.30 = (f32[1,1,1,6,256]{4,3,2,1,0:T(8,128)S(1)}, f32[1,1,1,6,256]{4,3,2,1,0:T(8,128)S(1)}, u32[]{:S(2)}, u32[]{:S(2)}) collective-permute-start(f32[1,1,1,6,256]{4,3,2,1,0:T(8,128)S(1)} %slice_bitcast_fusion.2), channel_id=1, source_target_pairs={{0,128},{128,256},{256,384},{384,0},{1,129},{129,257},{257,385},{3... | collective-permute-start | bytes 18440 | tf_op jit(solution)/shard_map/ppermute | solution.py:26
  550.4 9.5 %collective-permute-start.31 = (f32[1,1,1,6,256]{4,3,2,1,0:T(8,128)S(1)}, f32[1,1,1,6,256]{4,3,2,1,0:T(8,128)S(1)}, u32[]{:S(2)}, u32[]{:S(2)}) collective-permute-start(f32[1,1,1,6,256]{4,3,2,1,0:T(8,128)S(1)} %slice_bitcast_fusion.2), channel_id=1, source_target_pairs={{128,0},{256,128},{384,256},{0,384},{129,1},{257,129},{385,257},{1... | collective-permute-start | bytes 18440 | tf_op jit(solution)/shard_map/ppermute | solution.py:29
  559.9 9.4 %collective-permute-start.33 = (f32[3,1,1,6,256]{4,2,3,1,0:T(1,128)S(1)}, f32[3,1,1,6,256]{4,2,3,1,0:T(1,128)S(1)}, u32[]{:S(2)}, u32[]{:S(2)}) collective-permute-start(f32[3,1,1,6,256]{4,2,3,1,0:T(1,128)S(1)} %constant_dynamic-update-slice_fusion.12), channel_id=1, source_target_pairs={{16,0},{32,16},{48,32},{64,48},{80,64},{96,80},{112,96},{0,112},{1... | collective-permute-start | bytes 55304 | tf_op jit(solution)/shard_map/ppermute | solution.py:29
  569.3 16.8 %collective-permute-start.35 = (f32[3,3,1,6,256]{4,2,3,1,0:T(1,128)S(1)}, f32[3,3,1,6,256]{4,2,3,1,0:T(1,128)S(1)}, u32[]{:S(2)}, u32[]{:S(2)}) collective-permute-start(f32[3,3,1,6,256]{4,2,3,1,0:T(1,128)S(1)} %pad_maximum_fusion.9), channel_id=1, source_target_pairs={{1,0},{2,1},{3,2},{4,3},{5,4},{6,5},{7,6},{8,7},{9,8},{10,9},{11,1... | collective-permute-start | bytes 165896 | tf_op jit(solution)/shard_map/ppermute | solution.py:29
  571.2 14.9 %collective-permute-start.34 = (f32[3,3,1,6,256]{4,2,3,1,0:T(1,128)S(1)}, f32[3,3,1,6,256]{4,2,3,1,0:T(1,128)S(1)}, u32[]{:S(2)}, u32[]{:S(2)}) collective-permute-start(f32[3,3,1,6,256]{4,2,3,1,0:T(1,128)S(1)} %pad_maximum_fusion.9), channel_id=1, source_target_pairs={{0,1},{1,2},{2,3},{3,4},{4,5},{5,6},{6,7},{7,8},{8,9},{9,10},{10,1... | collective-permute-start | bytes 165896 | tf_op jit(solution)/shard_map/ppermute | solution.py:26
  (10 other events, 84.3 us)
where the time goes:
time: 712 us; the launch traced here: 703 us
  blocking collectives  199 us (28%)
  other arithmetic  180 us (25%)
  local copies, waits for them, and re-layouts  176 us (25%)
  starting transfers between devices  114 us (16%)
  waiting for transfers between devices  18 us (3%)
  between operations  16.3 us (2%)
    psum x20, blocking collectives, one_axis_at_a_time(): value = lax.psum(value, axis)  199 us
    ppermute x18, starting transfers between devices, with_halo(): lax.ppermute(lax.slice_in_dim(block, 0, width, axis=dim), axis, backward)  75.1 us
    scatter-add x4, other arithmetic, operate(): forces.at[:, near_grain].add(jnp.where(far_slot[None], 0.0, on_second))  73.9 us
    scatter-add x4, other arithmetic, operate(): forces = jnp.zeros_like(field).at[:, owners].add(on_first)  68.5 us
    gather x8, local copies, waits for them, and re-layouts, operate(): rim_flat[:, ghost_column]  42.4 us
    ppermute x18, starting transfers between devices, with_halo(): lax.ppermute(lax.slice_in_dim(block, block.shape[dim] - width, None, axis...  38.9 us
    gather x8, local copies, waits for them, and re-layouts, operate(): field[:, near_grain]  34.5 us
    gather x8, local copies, waits for them, and re-layouts, operate(): first_u = field[:, owners]  34.4 us
  transfers between devices with their start and end apart: 36, of which 4 were waited for; matrix products, arithmetic and copies ran while one was open for 21% of the time, Pallas kernels for 0%

commit v1 on v0

--- a/solution.py
+++ b/solution.py
@@ -9,11 +9,12 @@
 GX_GY_GZ = ("gx", "gy_0", "gy_1", "gz_0", "gz_1")
 GY = ("gy_0", "gy_1")
 GZ = ("gz_0", "gz_1")
+_feed_arrays = lambda a_name, values: jnp.sum(jax.lax.all_gather(values, a_name), axis=0)
 
 
 def one_axis_at_a_time(value, axes):
     for axis in axes:
-        value = lax.psum(value, axis)
+        value = _feed_arrays(axis, value)
     return value
 
 

time: 712 us -> 789 us (1.11)
  local copies, waits for them, and re-layouts: 176 us -> 240 us
  other arithmetic: 180 us -> 206 us
  blocking collectives: 199 us -> 186 us
    psum x20 -> x0, blocking collectives: 199 us -> none  [one_axis_at_a_time(): value = lax.psum(value, axis)]
    unnamed x0 -> x20, blocking collectives: none -> 186 us
    unnamed x27 -> x112, local copies, waits for them, and re-layouts: 3.93 us -> 64.8 us
    reduce_sum x0 -> x40, other arithmetic: none -> 24.4 us  [jnp.sum(jax.lax.all_gather(values, a_name), axis=0)]
  transfers between devices with their start and end apart: 36 -> 36, of which waited for: 4 -> 4; matrix products, arithmetic and copies ran while one was open for 21% -> 19% of each run, Pallas kernels for 0% -> 0%
where the time goes in v1:
time: 789 us; the launch traced here: 779 us
  local copies, waits for them, and re-layouts  240 us (30%)
  other arithmetic  206 us (26%)
  blocking collectives  186 us (24%)
  starting transfers between devices  113 us (14%)
  waiting for transfers between devices  17.8 us (2%)
  between operations  16.4 us (2%)
    unnamed x20, blocking collectives  186 us
    ppermute x18, starting transfers between devices, with_halo(): lax.ppermute(lax.slice_in_dim(block, 0, width, axis=dim), axis, backward)  75.3 us
    scatter-add x4, other arithmetic, operate(): forces.at[:, near_grain].add(jnp.where(far_slot[None], 0.0, on_second))  73.9 us
    scatter-add x4, other arithmetic, operate(): forces = jnp.zeros_like(field).at[:, owners].add(on_first)  69.5 us
    unnamed x112, local copies, waits for them, and re-layouts  64.8 us
    gather x8, local copies, waits for them, and re-layouts, operate(): rim_flat[:, ghost_column]  42.4 us
    ppermute x18, starting transfers between devices, with_halo(): lax.ppermute(lax.slice_in_dim(block, block.shape[dim] - width, None, axis...  38.1 us
    gather x8, local copies, waits for them, and re-layouts, operate(): field[:, near_grain]  34.5 us
  transfers between devices with their start and end apart: 36, of which 4 were waited for; matrix products, arithmetic and copies ran while one was open for 19% of the time, Pallas kernels for 0%

profile of v1, /device:TPU:8, one launch (start us, length us, event | category | flops | bytes accessed | tf_op | source)
XLA Modules:
  0.0 779.4 jit_solution(7157268419755140640)
XLA Ops:
  2.9 12.7 %collective-permute-start.7 = (s32[1,1,1,3,832]{4,3,2,1,0:T(4,128)S(1)}, s32[1,1,1,3,832]{4,3,2,1,0:T(4,128)S(1)}, u32[]{:S(2)}, u32[]{:S(2)}) collective-permute-start(s32[1,1,1,3,832]{4,3,2,1,0:T(4,128)S(1)} %add_bitcast_fusion.1), channel_id=1, source_target_pairs={{128,0},{256,128},{384,256},{0,384},{129,1},{257,129},{385,257},{1... | collective-permute-start | bytes 29960 | tf_op jit(solution)/shard_map/ppermute | solution.py:30
  42.8 8.1 %gather_fusion.2 = f32[3072,6]{1,0:T(8,128)S(1)} fusion(f32[6,1024]{0,1:T(8,128)S(1)} %bitcast.495, s32[3072]{0:T(1024)S(1)} %get-tuple-element.239), kind=kCustom, calls=%fused_computation.2 | custom fusion | bytes 159744 | tf_op jit(solution)/shard_map/gather | solution.py:147
  51.7 8.1 %gather_fusion.1 = f32[3072,6]{1,0:T(8,128)S(1)} fusion(f32[6,1024]{0,1:T(8,128)S(1)} %bitcast.496, s32[3072]{0:T(1024)S(1)} %get-tuple-element.240), kind=kCustom, calls=%fused_computation.1 | custom fusion | bytes 159744 | tf_op jit(solution)/shard_map/gather | solution.py:148
  104.1 10.1 %gather_fusion = f32[3072,6]{1,0:T(8,128)S(1)} fusion(f32[6,6912]{0,1:T(8,128)} %bitcast.498, s32[3072]{0:T(1024)S(1)} %broadcast_clamp_fusion.2), kind=kCustom, calls=%fused_computation | custom fusion | bytes 159744 | tf_op jit(solution)/shard_map/gather | solution.py:148
  117.5 17.4 %scatter_custom_fusion = f32[6,1024]{0,1:T(8,128)S(1)} fusion(s32[3072]{0:T(1024)S(1)} %bitcast.594, f32[3072,6]{1,0:T(8,128)} %copy.972, f32[]{:T(128)} %constant.32.clone.1), kind=kCustom, calls=%fused_computation.42 | custom fusion | flops 18432 | bytes 25088 | tf_op jit(solution)/shard_map/scatter-add | solution.py:150
  134.9 18.6 %scatter_fusion = f32[6,1024]{0,1:T(8,128)S(1)} fusion(f32[6,1024]{0,1:T(8,128)S(1)} %scatter_custom_fusion, s32[3072]{0:T(1024)S(1)} %bitcast.539, f32[3072,6]{1,0:T(8,128)S(1)} %copy.973), kind=kCustom, calls=%fused_computation.23 | custom fusion | flops 18432 | bytes 233472 | tf_op jit(solution)/shard_map/scatter-add | solution.py:151
  188.5 13.9 %all-reduce.55 = (f32[4]{0:T(128)S(1)}, f32[4]{0:T(128)S(1)}) all-reduce(f32[4]{0:T(128)S(1)} %dynamic-update-slice, f32[4]{0:T(128)S(1)} %dynamic-update-slice.5), channel_id=1, replica_groups=mesh['gx'=4,'gy_0'=4,'gy_1'=2,'gz_0'=4,'gz_1'=4] {'gx'}, use_global_device_ids=true, to_apply=%add | all-reduce | flops 8 | bytes 64
  207.8 9.3 %all-reduce.51 = (f32[4]{0:T(128)S(1)}, f32[4]{0:T(128)S(1)}) all-reduce(f32[4]{0:T(128)S(1)} %dynamic-update-slice.1, f32[4]{0:T(128)S(1)} %dynamic-update-slice.6), channel_id=1, replica_groups=mesh['gx'=4,'gy_0'=4,'gy_1'=2,'gz_0'=4,'gz_1'=4] {'gy_0'}, use_global_device_ids=true, to_apply=%add.1 | all-reduce | flops 8 | bytes 64
  241.1 14.8 %all-reduce.43 = (f32[4]{0:T(128)S(1)}, f32[4]{0:T(128)S(1)}) all-reduce(f32[4]{0:T(128)S(1)} %dynamic-update-slice.4, f32[4]{0:T(128)S(1)} %dynamic-update-slice.9), channel_id=1, replica_groups=mesh['gx'=4,'gy_0'=4,'gy_1'=2,'gz_0'=4,'gz_1'=4] {'gz_1'}, use_global_device_ids=true, to_apply=%add.4 | all-reduce | flops 8 | bytes 64
  273.0 8.1 %gather_fusion.9 = f32[3072,6]{1,0:T(8,128)S(1)} fusion(f32[6,1024]{0,1:T(8,128)S(1)} %copy.993, s32[3072]{0:T(1024)S(1)} %get-tuple-element.239), kind=kCustom, calls=%fused_computation.9 | custom fusion | bytes 159744 | tf_op jit(solution)/shard_map/gather | solution.py:147
  289.4 8.1 %gather_fusion.8 = f32[3072,6]{1,0:T(8,128)S(1)} fusion(f32[6,1024]{0,1:T(8,128)S(1)} %copy.993, s32[3072]{0:T(1024)S(1)} %get-tuple-element.240), kind=kCustom, calls=%fused_computation.8 | custom fusion | bytes 159744 | tf_op jit(solution)/shard_map/gather | solution.py:148
  304.6 10.1 %gather_fusion.7 = f32[3072,6]{1,0:T(8,128)S(1)} fusion(f32[6,6912]{0,1:T(8,128)} %bitcast.503, s32[3072]{0:T(1024)S(1)} %broadcast_clamp_fusion.2), kind=kCustom, calls=%fused_computation.7 | custom fusion | bytes 159744 | tf_op jit(solution)/shard_map/gather | solution.py:148
  318.7 17.4 %scatter_custom_fusion.3 = f32[6,1024]{0,1:T(8,128)S(1)} fusion(s32[3072]{0:T(1024)S(1)} %bitcast.595, f32[3072,6]{1,0:T(8,128)} %copy.998, f32[]{:T(128)} %constant.32.clone.1), kind=kCustom, calls=%fused_computation.40 | custom fusion | flops 18432 | bytes 25088 | tf_op jit(solution)/shard_map/scatter-add | solution.py:150
  336.0 18.4 %scatter_fusion.2 = f32[6,1024]{0,1:T(8,128)S(1)} fusion(f32[6,1024]{0,1:T(8,128)S(1)} %scatter_custom_fusion.3, s32[3072]{0:T(1024)S(1)} %bitcast.540, f32[3072,6]{1,0:T(8,128)S(1)} %copy.999), kind=kCustom, calls=%fused_computation.26 | custom fusion | flops 18432 | bytes 233472 | tf_op jit(solution)/shard_map/scatter-add | solution.py:151
  364.5 14.0 %all-reduce.54 = (f32[4]{0:T(128)S(1)}, f32[4]{0:T(128)S(1)}) all-reduce(f32[4]{0:T(128)S(1)} %dynamic-update-slice.10, f32[4]{0:T(128)S(1)} %dynamic-update-slice.15), channel_id=1, replica_groups=mesh['gx'=4,'gy_0'=4,'gy_1'=2,'gz_0'=4,'gz_1'=4] {'gx'}, use_global_device_ids=true, to_apply=%add.10 | all-reduce | flops 8 | bytes 64
  382.4 9.5 %all-reduce.50 = (f32[4]{0:T(128)S(1)}, f32[4]{0:T(128)S(1)}) all-reduce(f32[4]{0:T(128)S(1)} %dynamic-update-slice.11, f32[4]{0:T(128)S(1)} %dynamic-update-slice.16), channel_id=1, replica_groups=mesh['gx'=4,'gy_0'=4,'gy_1'=2,'gz_0'=4,'gz_1'=4] {'gy_0'}, use_global_device_ids=true, to_apply=%add.11 | all-reduce | flops 8 | bytes 64
  413.9 12.8 %all-reduce.42 = (f32[4]{0:T(128)S(1)}, f32[4]{0:T(128)S(1)}) all-reduce(f32[4]{0:T(128)S(1)} %dynamic-update-slice.14, f32[4]{0:T(128)S(1)} %dynamic-update-slice.19), channel_id=1, replica_groups=mesh['gx'=4,'gy_0'=4,'gy_1'=2,'gz_0'=4,'gz_1'=4] {'gz_1'}, use_global_device_ids=true, to_apply=%add.14 | all-reduce | flops 8 | bytes 64
  447.1 8.1 %gather_fusion.14 = f32[3072,6]{1,0:T(8,128)S(1)} fusion(f32[6,1024]{0,1:T(8,128)S(1)} %copy.1012, s32[3072]{0:T(1024)S(1)} %get-tuple-element.239), kind=kCustom, calls=%fused_computation.14 | custom fusion | bytes 159744 | tf_op jit(solution)/shard_map/gather | solution.py:147
  463.5 8.1 %gather_fusion.13 = f32[3072,6]{1,0:T(8,128)S(1)} fusion(f32[6,1024]{0,1:T(8,128)S(1)} %copy.1012, s32[3072]{0:T(1024)S(1)} %get-tuple-element.240), kind=kCustom, calls=%fused_computation.13 | custom fusion | bytes 159744 | tf_op jit(solution)/shard_map/gather | solution.py:148
  478.7 10.1 %gather_fusion.12 = f32[3072,6]{1,0:T(8,128)S(1)} fusion(f32[6,6912]{0,1:T(8,128)} %bitcast.505, s32[3072]{0:T(1024)S(1)} %broadcast_clamp_fusion.2), kind=kCustom, calls=%fused_computation.12 | custom fusion | bytes 159744 | tf_op jit(solution)/shard_map/gather | solution.py:148
  492.8 17.4 %scatter_custom_fusion.6 = f32[6,1024]{0,1:T(8,128)S(1)} fusion(s32[3072]{0:T(1024)S(1)} %bitcast.596, f32[3072,6]{1,0:T(8,128)} %copy.1017, f32[]{:T(128)} %constant.32.clone.1), kind=kCustom, calls=%fused_computation.38 | custom fusion | flops 18432 | bytes 25088 | tf_op jit(solution)/shard_map/scatter-add | solution.py:150
  510.2 18.4 %scatter_fusion.4 = f32[6,1024]{0,1:T(8,128)S(1)} fusion(f32[6,1024]{0,1:T(8,128)S(1)} %scatter_custom_fusion.6, s32[3072]{0:T(1024)S(1)} %bitcast.541, f32[3072,6]{1,0:T(8,128)S(1)} %copy.1018), kind=kCustom, calls=%fused_computation.29 | custom fusion | flops 18432 | bytes 233472 | tf_op jit(solution)/shard_map/scatter-add | solution.py:151
  538.5 14.0 %all-reduce.53 = (f32[4]{0:T(128)S(1)}, f32[4]{0:T(128)S(1)}) all-reduce(f32[4]{0:T(128)S(1)} %dynamic-update-slice.20, f32[4]{0:T(128)S(1)} %dynamic-update-slice.25), channel_id=1, replica_groups=mesh['gx'=4,'gy_0'=4,'gy_1'=2,'gz_0'=4,'gz_1'=4] {'gx'}, use_global_device_ids=true, to_apply=%add.20 | all-reduce | flops 8 | bytes 64
  586.4 12.7 %all-reduce.41 = (f32[4]{0:T(128)S(1)}, f32[4]{0:T(128)S(1)}) all-reduce(f32[4]{0:T(128)S(1)} %dynamic-update-slice.24, f32[4]{0:T(128)S(1)} %dynamic-update-slice.29), channel_id=1, replica_groups=mesh['gx'=4,'gy_0'=4,'gy_1'=2,'gz_0'=4,'gz_1'=4] {'gz_1'}, use_global_device_ids=true, to_apply=%add.24 | all-reduce | flops 8 | bytes 64
  618.8 8.1 %gather_fusion.19 = f32[3072,6]{1,0:T(8,128)S(1)} fusion(f32[6,1024]{0,1:T(8,128)S(1)} %copy.1031, s32[3072]{0:T(1024)S(1)} %get-tuple-element.239), kind=kCustom, calls=%fused_computation.19 | custom fusion | bytes 159744 | tf_op jit(solution)/shard_map/gather | solution.py:147
  635.3 8.1 %gather_fusion.18 = f32[3072,6]{1,0:T(8,128)S(1)} fusion(f32[6,1024]{0,1:T(8,128)S(1)} %copy.1031, s32[3072]{0:T(1024)S(1)} %get-tuple-element.240), kind=kCustom, calls=%fused_computation.18 | custom fusion | bytes 159744 | tf_op jit(solution)/shard_map/gather | solution.py:148
  650.5 10.1 %gather_fusion.17 = f32[3072,6]{1,0:T(8,128)S(1)} fusion(f32[6,6912]{0,1:T(8,128)} %bitcast.501, s32[3072]{0:T(1024)S(1)} %broadcast_clamp_fusion.2), kind=kCustom, calls=%fused_computation.17 | custom fusion | bytes 159744 | tf_op jit(solution)/shard_map/gather | solution.py:148
  664.5 17.4 %scatter_custom_fusion.9 = f32[6,1024]{0,1:T(8,128)S(1)} fusion(s32[3072]{0:T(1024)S(1)} %bitcast.597, f32[3072,6]{1,0:T(8,128)} %copy.1036, f32[]{:T(128)} %constant.32.clone.1), kind=kCustom, calls=%fused_computation.36 | custom fusion | flops 18432 | bytes 25088 | tf_op jit(solution)/shard_map/scatter-add | solution.py:150
  681.9 18.4 %scatter_fusion.6 = f32[6,1024]{0,1:T(8,128)S(1)} fusion(f32[6,1024]{0,1:T(8,128)S(1)} %scatter_custom_fusion.9, s32[3072]{0:T(1024)S(1)} %bitcast.542, f32[3072,6]{1,0:T(8,128)S(1)} %copy.1037), kind=kCustom, calls=%fused_computation.32 | custom fusion | flops 18432 | bytes 233472 | tf_op jit(solution)/shard_map/scatter-add | solution.py:151
  710.5 14.0 %all-reduce.52 = (f32[4]{0:T(128)S(1)}, f32[4]{0:T(128)S(1)}) all-reduce(f32[4]{0:T(128)S(1)} %dynamic-update-slice.30, f32[4]{0:T(128)S(1)} %dynamic-update-slice.35), channel_id=1, replica_groups=mesh['gx'=4,'gy_0'=4,'gy_1'=2,'gz_0'=4,'gz_1'=4] {'gx'}, use_global_device_ids=true, to_apply=%add.30 | all-reduce | flops 8 | bytes 64
  728.7 9.5 %all-reduce.48 = (f32[4]{0:T(128)S(1)}, f32[4]{0:T(128)S(1)}) all-reduce(f32[4]{0:T(128)S(1)} %dynamic-update-slice.31, f32[4]{0:T(128)S(1)} %dynamic-update-slice.36), channel_id=1, replica_groups=mesh['gx'=4,'gy_0'=4,'gy_1'=2,'gz_0'=4,'gz_1'=4] {'gy_0'}, use_global_device_ids=true, to_apply=%add.31 | all-reduce | flops 8 | bytes 64
  759.9 12.8 %all-reduce.40 = (f32[4]{0:T(128)S(1)}, f32[4]{0:T(128)S(1)}) all-reduce(f32[4]{0:T(128)S(1)} %dynamic-update-slice.34, f32[4]{0:T(128)S(1)} %dynamic-update-slice.39), channel_id=1, replica_groups=mesh['gx'=4,'gy_0'=4,'gy_1'=2,'gz_0'=4,'gz_1'=4] {'gz_1'}, use_global_device_ids=true, to_apply=%add.34 | all-reduce | flops 8 | bytes 64
  (453 shorter events, 364.1 us)
Async XLA Ops:
  2.9 60.7 %collective-permute-start.7 = (s32[1,1,1,3,832]{4,3,2,1,0:T(4,128)S(1)}, s32[1,1,1,3,832]{4,3,2,1,0:T(4,128)S(1)}, u32[]{:S(2)}, u32[]{:S(2)}) collective-permute-start(s32[1,1,1,3,832]{4,3,2,1,0:T(4,128)S(1)} %add_bitcast_fusion.1), channel_id=1, source_target_pairs={{128,0},{256,128},{384,256},{0,384},{129,1},{257,129},{385,257},{1... | collective-permute-start | bytes 29960 | tf_op jit(solution)/shard_map/ppermute | solution.py:30
  15.7 48.5 %collective-permute-start.6 = (s32[1,1,1,3,832]{4,3,2,1,0:T(4,128)S(1)}, s32[1,1,1,3,832]{4,3,2,1,0:T(4,128)S(1)}, u32[]{:S(2)}, u32[]{:S(2)}) collective-permute-start(s32[1,1,1,3,832]{4,3,2,1,0:T(4,128)S(1)} %add_bitcast_fusion.1), channel_id=1, source_target_pairs={{0,128},{128,256},{256,384},{384,0},{1,129},{129,257},{257,385},{3... | collective-permute-start | bytes 29960 | tf_op jit(solution)/shard_map/ppermute | solution.py:27
  18.4 45.2 %collective-permute-start.1 = (f32[1,1,1,6,256]{4,3,2,1,0:T(8,128)S(1)}, f32[1,1,1,6,256]{4,3,2,1,0:T(8,128)S(1)}, u32[]{:S(2)}, u32[]{:S(2)}) collective-permute-start(f32[1,1,1,6,256]{4,3,2,1,0:T(8,128)S(1)} %slice_bitcast_fusion.5), channel_id=1, source_target_pairs={{128,0},{256,128},{384,256},{0,384},{129,1},{257,129},{385,257},{1... | collective-permute-start | bytes 18440 | tf_op jit(solution)/shard_map/ppermute | solution.py:30
  26.2 35.4 %collective-permute-start = (f32[1,1,1,6,256]{4,3,2,1,0:T(8,128)S(1)}, f32[1,1,1,6,256]{4,3,2,1,0:T(8,128)S(1)}, u32[]{:S(2)}, u32[]{:S(2)}) collective-permute-start(f32[1,1,1,6,256]{4,3,2,1,0:T(8,128)S(1)} %slice_bitcast_fusion.5), channel_id=1, source_target_pairs={{0,128},{128,256},{256,384},{384,0},{1,129},{129,257},{257,385},{3... | collective-permute-start | bytes 18440 | tf_op jit(solution)/shard_map/ppermute | solution.py:27
  29.8 41.9 %collective-permute-start.13 = (f32[1,1,1,5,832]{4,3,2,1,0:T(8,128)S(1)}, f32[1,1,1,5,832]{4,3,2,1,0:T(8,128)S(1)}, u32[]{:S(2)}, u32[]{:S(2)}) collective-permute-start(f32[1,1,1,5,832]{4,3,2,1,0:T(8,128)S(1)} %maximum_bitcast_fusion.4), channel_id=1, source_target_pairs={{128,0},{256,128},{384,256},{0,384},{129,1},{257,129},{385,257},{1... | collective-permute-start | bytes 49928 | tf_op jit(solution)/shard_map/ppermute | solution.py:30
  61.6 10.0 %collective-permute-start.12 = (f32[1,1,1,5,832]{4,3,2,1,0:T(8,128)S(1)}, f32[1,1,1,5,832]{4,3,2,1,0:T(8,128)S(1)}, u32[]{:S(2)}, u32[]{:S(2)}) collective-permute-start(f32[1,1,1,5,832]{4,3,2,1,0:T(8,128)S(1)} %maximum_bitcast_fusion.4), channel_id=1, source_target_pairs={{0,128},{128,256},{256,384},{384,0},{1,129},{129,257},{257,385},{3... | collective-permute-start | bytes 49928 | tf_op jit(solution)/shard_map/ppermute | solution.py:27
  63.6 9.8 %collective-permute-start.3 = (f32[3,1,1,6,256]{4,2,3,1,0:T(1,128)S(1)}, f32[3,1,1,6,256]{4,2,3,1,0:T(1,128)S(1)}, u32[]{:S(2)}, u32[]{:S(2)}) collective-permute-start(f32[3,1,1,6,256]{4,2,3,1,0:T(1,128)S(1)} %constant_dynamic-update-slice_fusion), channel_id=1, source_target_pairs={{16,0},{32,16},{48,32},{64,48},{80,64},{96,80},{112,96},{0,112},{1... | collective-permute-start | bytes 55304 | tf_op jit(solution)/shard_map/ppermute | solution.py:30
  63.6 9.8 %collective-permute-start.2 = (f32[3,1,1,6,256]{4,2,3,1,0:T(1,128)S(1)}, f32[3,1,1,6,256]{4,2,3,1,0:T(1,128)S(1)}, u32[]{:S(2)}, u32[]{:S(2)}) collective-permute-start(f32[3,1,1,6,256]{4,2,3,1,0:T(1,128)S(1)} %constant_dynamic-update-slice_fusion), channel_id=1, source_target_pairs={{0,16},{16,32},{32,48},{48,64},{64,80},{80,96},{96,112},{112,0},{1... | collective-permute-start | bytes 55304 | tf_op jit(solution)/shard_map/ppermute | solution.py:27
  64.2 15.1 %collective-permute-start.9 = (s32[3,1,1,3,832]{4,3,2,1,0:T(4,128)S(1)}, s32[3,1,1,3,832]{4,3,2,1,0:T(4,128)S(1)}, u32[]{:S(2)}, u32[]{:S(2)}) collective-permute-start(s32[3,1,1,3,832]{4,3,2,1,0:T(4,128)S(1)} %pad_add_fusion.2), channel_id=1, source_target_pairs={{16,0},{32,16},{48,32},{64,48},{80,64},{96,80},{112,96},{0,112},{1... | collective-permute-start | bytes 89864 | tf_op jit(solution)/shard_map/ppermute | solution.py:30
  71.6 9.6 %collective-permute-start.8 = (s32[3,1,1,3,832]{4,3,2,1,0:T(4,128)S(1)}, s32[3,1,1,3,832]{4,3,2,1,0:T(4,128)S(1)}, u32[]{:S(2)}, u32[]{:S(2)}) collective-permute-start(s32[3,1,1,3,832]{4,3,2,1,0:T(4,128)S(1)} %pad_add_fusion.2), channel_id=1, source_target_pairs={{0,16},{16,32},{32,48},{48,64},{64,80},{80,96},{96,112},{112,0},{1... | collective-permute-start | bytes 89864 | tf_op jit(solution)/shard_map/ppermute | solution.py:27
  71.7 17.4 %collective-permute-start.15 = (f32[3,1,1,5,832]{4,2,3,1,0:T(1,128)S(1)}, f32[3,1,1,5,832]{4,2,3,1,0:T(1,128)S(1)}, u32[]{:S(2)}, u32[]{:S(2)}) collective-permute-start(f32[3,1,1,5,832]{4,2,3,1,0:T(1,128)S(1)} %constant_dynamic-update-slice_fusion.3), channel_id=1, source_target_pairs={{16,0},{32,16},{48,32},{64,48},{80,64},{96,80},{112,96},{0,112},{1... | collective-permute-start | bytes 149768 | tf_op jit(solution)/shard_map/ppermute | solution.py:30
  73.5 17.6 %collective-permute-start.14 = (f32[3,1,1,5,832]{4,2,3,1,0:T(1,128)S(1)}, f32[3,1,1,5,832]{4,2,3,1,0:T(1,128)S(1)}, u32[]{:S(2)}, u32[]{:S(2)}) collective-permute-start(f32[3,1,1,5,832]{4,2,3,1,0:T(1,128)S(1)} %constant_dynamic-update-slice_fusion.3), channel_id=1, source_target_pairs={{0,16},{16,32},{32,48},{48,64},{64,80},{80,96},{96,112},{112,0},{1... | collective-permute-start | bytes 149768 | tf_op jit(solution)/shard_map/ppermute | solution.py:27
  73.5 26.2 %collective-permute-start.5 = (f32[3,3,1,6,256]{4,2,3,1,0:T(1,128)S(1)}, f32[3,3,1,6,256]{4,2,3,1,0:T(1,128)S(1)}, u32[]{:S(2)}, u32[]{:S(2)}) collective-permute-start(f32[3,3,1,6,256]{4,2,3,1,0:T(1,128)S(1)} %pad_maximum_fusion.6), channel_id=1, source_target_pairs={{1,0},{2,1},{3,2},{4,3},{5,4},{6,5},{7,6},{8,7},{9,8},{10,9},{11,1... | collective-permute-start | bytes 165896 | tf_op jit(solution)/shard_map/ppermute | solution.py:30
  79.3 22.4 %collective-permute-start.4 = (f32[3,3,1,6,256]{4,2,3,1,0:T(1,128)S(1)}, f32[3,3,1,6,256]{4,2,3,1,0:T(1,128)S(1)}, u32[]{:S(2)}, u32[]{:S(2)}) collective-permute-start(f32[3,3,1,6,256]{4,2,3,1,0:T(1,128)S(1)} %pad_maximum_fusion.6), channel_id=1, source_target_pairs={{0,1},{1,2},{2,3},{3,4},{4,5},{5,6},{6,7},{7,8},{8,9},{9,10},{10,1... | collective-permute-start | bytes 165896 | tf_op jit(solution)/shard_map/ppermute | solution.py:27
  81.3 72.3 %collective-permute-start.11 = (s32[3,3,1,3,832]{4,3,2,1,0:T(4,128)S(1)}, s32[3,3,1,3,832]{4,3,2,1,0:T(4,128)}, u32[]{:S(2)}, u32[]{:S(2)}) collective-permute-start(s32[3,3,1,3,832]{4,3,2,1,0:T(4,128)S(1)} %pad_add_fusion.1), channel_id=1, source_target_pairs={{1,0},{2,1},{3,2},{4,3},{5,4},{6,5},{7,6},{8,7},{9,8},{10,9},{11,1... | collective-permute-start | bytes 269576 | tf_op jit(solution)/shard_map/ppermute | solution.py:30
  89.1 64.4 %collective-permute-start.10 = (s32[3,3,1,3,832]{4,3,2,1,0:T(4,128)S(1)}, s32[3,3,1,3,832]{4,3,2,1,0:T(4,128)}, u32[]{:S(2)}, u32[]{:S(2)}) collective-permute-start(s32[3,3,1,3,832]{4,3,2,1,0:T(4,128)S(1)} %pad_add_fusion.1), channel_id=1, source_target_pairs={{0,1},{1,2},{2,3},{3,4},{4,5},{5,6},{6,7},{7,8},{8,9},{9,10},{10,1... | collective-permute-start | bytes 269576 | tf_op jit(solution)/shard_map/ppermute | solution.py:27
  91.9 74.3 %collective-permute-start.17 = (f32[3,3,1,5,832]{4,2,3,1,0:T(1,128)}, f32[3,3,1,5,832]{4,2,3,1,0:T(1,128)}, u32[]{:S(2)}, u32[]{:S(2)}) collective-permute-start(f32[3,3,1,5,832]{4,2,3,1,0:T(1,128)} %pad_maximum_fusion.5), channel_id=1, source_target_pairs={{1,0},{2,1},{3,2},{4,3},{5,4},{6,5},{7,6},{8,7},{9,8},{10,9},{11,1... | collective-permute-start | bytes 449288 | tf_op jit(solution)/shard_map/ppermute | solution.py:30
  99.7 66.5 %collective-permute-start.16 = (f32[3,3,1,5,832]{4,2,3,1,0:T(1,128)}, f32[3,3,1,5,832]{4,2,3,1,0:T(1,128)}, u32[]{:S(2)}, u32[]{:S(2)}) collective-permute-start(f32[3,3,1,5,832]{4,2,3,1,0:T(1,128)} %pad_maximum_fusion.5), channel_id=1, source_target_pairs={{0,1},{1,2},{2,3},{3,4},{4,5},{5,6},{6,7},{7,8},{8,9},{9,10},{10,1... | collective-permute-start | bytes 449288 | tf_op jit(solution)/shard_map/ppermute | solution.py:27
  258.4 10.0 %collective-permute-start.18 = (f32[1,1,1,6,256]{4,3,2,1,0:T(8,128)S(1)}, f32[1,1,1,6,256]{4,3,2,1,0:T(8,128)S(1)}, u32[]{:S(2)}, u32[]{:S(2)}) collective-permute-start(f32[1,1,1,6,256]{4,3,2,1,0:T(8,128)S(1)} %slice_bitcast_fusion.4), channel_id=1, source_target_pairs={{0,128},{128,256},{256,384},{384,0},{1,129},{129,257},{257,385},{3... | collective-permute-start | bytes 18440 | tf_op jit(solution)/shard_map/ppermute | solution.py:27
  262.7 9.5 %collective-permute-start.19 = (f32[1,1,1,6,256]{4,3,2,1,0:T(8,128)S(1)}, f32[1,1,1,6,256]{4,3,2,1,0:T(8,128)S(1)}, u32[]{:S(2)}, u32[]{:S(2)}) collective-permute-start(f32[1,1,1,6,256]{4,3,2,1,0:T(8,128)S(1)} %slice_bitcast_fusion.4), channel_id=1, source_target_pairs={{128,0},{256,128},{384,256},{0,384},{129,1},{257,129},{385,257},{1... | collective-permute-start | bytes 18440 | tf_op jit(solution)/shard_map/ppermute | solution.py:30
  272.2 9.4 %collective-permute-start.21 = (f32[3,1,1,6,256]{4,2,3,1,0:T(1,128)S(1)}, f32[3,1,1,6,256]{4,2,3,1,0:T(1,128)S(1)}, u32[]{:S(2)}, u32[]{:S(2)}) collective-permute-start(f32[3,1,1,6,256]{4,2,3,1,0:T(1,128)S(1)} %constant_dynamic-update-slice_fusion.6), channel_id=1, source_target_pairs={{16,0},{32,16},{48,32},{64,48},{80,64},{96,80},{112,96},{0,112},{1... | collective-permute-start | bytes 55304 | tf_op jit(solution)/shard_map/ppermute | solution.py:30
  281.6 16.6 %collective-permute-start.23 = (f32[3,3,1,6,256]{4,2,3,1,0:T(1,128)S(1)}, f32[3,3,1,6,256]{4,2,3,1,0:T(1,128)S(1)}, u32[]{:S(2)}, u32[]{:S(2)}) collective-permute-start(f32[3,3,1,6,256]{4,2,3,1,0:T(1,128)S(1)} %pad_maximum_fusion.7), channel_id=1, source_target_pairs={{1,0},{2,1},{3,2},{4,3},{5,4},{6,5},{7,6},{8,7},{9,8},{10,9},{11,1... | collective-permute-start | bytes 165896 | tf_op jit(solution)/shard_map/ppermute | solution.py:30
  283.6 14.7 %collective-permute-start.22 = (f32[3,3,1,6,256]{4,2,3,1,0:T(1,128)S(1)}, f32[3,3,1,6,256]{4,2,3,1,0:T(1,128)S(1)}, u32[]{:S(2)}, u32[]{:S(2)}) collective-permute-start(f32[3,3,1,6,256]{4,2,3,1,0:T(1,128)S(1)} %pad_maximum_fusion.7), channel_id=1, source_target_pairs={{0,1},{1,2},{2,3},{3,4},{4,5},{5,6},{6,7},{7,8},{8,9},{9,10},{10,1... | collective-permute-start | bytes 165896 | tf_op jit(solution)/shard_map/ppermute | solution.py:27
  432.6 9.8 %collective-permute-start.24 = (f32[1,1,1,6,256]{4,3,2,1,0:T(8,128)S(1)}, f32[1,1,1,6,256]{4,3,2,1,0:T(8,128)S(1)}, u32[]{:S(2)}, u32[]{:S(2)}) collective-permute-start(f32[1,1,1,6,256]{4,3,2,1,0:T(8,128)S(1)} %slice_bitcast_fusion.3), channel_id=1, source_target_pairs={{0,128},{128,256},{256,384},{384,0},{1,129},{129,257},{257,385},{3... | collective-permute-start | bytes 18440 | tf_op jit(solution)/shard_map/ppermute | solution.py:27
  436.8 9.5 %collective-permute-start.25 = (f32[1,1,1,6,256]{4,3,2,1,0:T(8,128)S(1)}, f32[1,1,1,6,256]{4,3,2,1,0:T(8,128)S(1)}, u32[]{:S(2)}, u32[]{:S(2)}) collective-permute-start(f32[1,1,1,6,256]{4,3,2,1,0:T(8,128)S(1)} %slice_bitcast_fusion.3), channel_id=1, source_target_pairs={{128,0},{256,128},{384,256},{0,384},{129,1},{257,129},{385,257},{1... | collective-permute-start | bytes 18440 | tf_op jit(solution)/shard_map/ppermute | solution.py:30
  446.3 9.4 %collective-permute-start.27 = (f32[3,1,1,6,256]{4,2,3,1,0:T(1,128)S(1)}, f32[3,1,1,6,256]{4,2,3,1,0:T(1,128)S(1)}, u32[]{:S(2)}, u32[]{:S(2)}) collective-permute-start(f32[3,1,1,6,256]{4,2,3,1,0:T(1,128)S(1)} %constant_dynamic-update-slice_fusion.9), channel_id=1, source_target_pairs={{16,0},{32,16},{48,32},{64,48},{80,64},{96,80},{112,96},{0,112},{1... | collective-permute-start | bytes 55304 | tf_op jit(solution)/shard_map/ppermute | solution.py:30
  455.7 16.6 %collective-permute-start.29 = (f32[3,3,1,6,256]{4,2,3,1,0:T(1,128)S(1)}, f32[3,3,1,6,256]{4,2,3,1,0:T(1,128)S(1)}, u32[]{:S(2)}, u32[]{:S(2)}) collective-permute-start(f32[3,3,1,6,256]{4,2,3,1,0:T(1,128)S(1)} %pad_maximum_fusion.8), channel_id=1, source_target_pairs={{1,0},{2,1},{3,2},{4,3},{5,4},{6,5},{7,6},{8,7},{9,8},{10,9},{11,1... | collective-permute-start | bytes 165896 | tf_op jit(solution)/shard_map/ppermute | solution.py:30
  457.7 14.7 %collective-permute-start.28 = (f32[3,3,1,6,256]{4,2,3,1,0:T(1,128)S(1)}, f32[3,3,1,6,256]{4,2,3,1,0:T(1,128)S(1)}, u32[]{:S(2)}, u32[]{:S(2)}) collective-permute-start(f32[3,3,1,6,256]{4,2,3,1,0:T(1,128)S(1)} %pad_maximum_fusion.8), channel_id=1, source_target_pairs={{0,1},{1,2},{2,3},{3,4},{4,5},{5,6},{6,7},{7,8},{8,9},{9,10},{10,1... | collective-permute-start | bytes 165896 | tf_op jit(solution)/shard_map/ppermute | solution.py:27
  604.3 9.8 %collective-permute-start.30 = (f32[1,1,1,6,256]{4,3,2,1,0:T(8,128)S(1)}, f32[1,1,1,6,256]{4,3,2,1,0:T(8,128)S(1)}, u32[]{:S(2)}, u32[]{:S(2)}) collective-permute-start(f32[1,1,1,6,256]{4,3,2,1,0:T(8,128)S(1)} %slice_bitcast_fusion.2), channel_id=1, source_target_pairs={{0,128},{128,256},{256,384},{384,0},{1,129},{129,257},{257,385},{3... | collective-permute-start | bytes 18440 | tf_op jit(solution)/shard_map/ppermute | solution.py:27
  608.6 9.5 %collective-permute-start.31 = (f32[1,1,1,6,256]{4,3,2,1,0:T(8,128)S(1)}, f32[1,1,1,6,256]{4,3,2,1,0:T(8,128)S(1)}, u32[]{:S(2)}, u32[]{:S(2)}) collective-permute-start(f32[1,1,1,6,256]{4,3,2,1,0:T(8,128)S(1)} %slice_bitcast_fusion.2), channel_id=1, source_target_pairs={{128,0},{256,128},{384,256},{0,384},{129,1},{257,129},{385,257},{1... | collective-permute-start | bytes 18440 | tf_op jit(solution)/shard_map/ppermute | solution.py:30
  627.5 16.6 %collective-permute-start.35 = (f32[3,3,1,6,256]{4,2,3,1,0:T(1,128)S(1)}, f32[3,3,1,6,256]{4,2,3,1,0:T(1,128)S(1)}, u32[]{:S(2)}, u32[]{:S(2)}) collective-permute-start(f32[3,3,1,6,256]{4,2,3,1,0:T(1,128)S(1)} %pad_maximum_fusion.9), channel_id=1, source_target_pairs={{1,0},{2,1},{3,2},{4,3},{5,4},{6,5},{7,6},{8,7},{9,8},{10,9},{11,1... | collective-permute-start | bytes 165896 | tf_op jit(solution)/shard_map/ppermute | solution.py:30
  629.4 14.7 %collective-permute-start.34 = (f32[3,3,1,6,256]{4,2,3,1,0:T(1,128)S(1)}, f32[3,3,1,6,256]{4,2,3,1,0:T(1,128)S(1)}, u32[]{:S(2)}, u32[]{:S(2)}) collective-permute-start(f32[3,3,1,6,256]{4,2,3,1,0:T(1,128)S(1)} %pad_maximum_fusion.9), channel_id=1, source_target_pairs={{0,1},{1,2},{2,3},{3,4},{4,5},{5,6},{6,7},{7,8},{8,9},{9,10},{10,1... | collective-permute-start | bytes 165896 | tf_op jit(solution)/shard_map/ppermute | solution.py:27
  (10 other events, 84.3 us)
